TPU v7x, 32 devices: a whole 2x2x4 slice. The times are simulated.
32 devices in a mesh: dp: 4 (over y, x), group: 8 (over z, core).
Axes of the slice: x: 2, y: 2, z: 4, core: 2. Of those that a mesh axis runs over, the one named last changes fastest.
Arguments:
- tokens: bfloat16 [2048, 5120], P('dp'), may hold values from -6 to 6
- frame_mask: int32 [2048], P('dp'), may hold values 0 or 1
- cotangent: bfloat16 [2048, 5120], P('dp'), may hold values from -0.625 to 0.625
- up_weight: bfloat16 [5120, 8192], P('dp', 'group'), may hold values from -0.078125 to 0.078125
- down_weight: bfloat16 [5120, 8192], P('dp', 'group'), may hold values from -0.0625 to 0.0625
- snap_params: bfloat16 [8, 32768], P(None, ('dp', 'group')), may hold values from -6 to 6
- first_moment: float32 [8, 32768], P(None, ('dp', 'group')), may hold values from -6 to 6
- second_moment: float32 [8, 32768], P(None, ('dp', 'group')), may hold values from 0.01 to 4
- range_of_writer: int32 [8], replicated, may hold values from 0 to 7, each once
Outputs:
- grad_up: float32 [5120, 8192], P('dp', 'group')
- grad_down: float32 [5120, 8192], P('dp', 'group')
- written_params: bfloat16 [8, 32768], P('group', 'dp')
- written_moments: float32 [2, 8, 32768], P(None, 'group', 'dp')
Inputs may be any that keep to these rules, and one draw needn't show every extreme that they name: `range_of_writer`: each of the 8 ranges is named by exactly one owner.
All inputs are finite; a program needn't handle non-finite values. No bound on the sum of `frame_mask` on one device may be relied on, other than what follows from the above.
Results may differ from a plain program's by a relative error of at most 0.017.
Values may be sent and summed in bfloat16 or wider, within the bound.
A program may use at most 128 MiB of HBM per device.

v0:
```python
import jax
import jax.numpy as jnp
from jax import lax
from jax.sharding import PartitionSpec as P

EPS = 1e-06


def normalize(tokens):
    values = tokens.astype(jnp.float32)
    centred = values - jnp.mean(values, axis=1, keepdims=True)
    spread = jnp.mean(centred * centred, axis=1, keepdims=True)
    return (centred * lax.rsqrt(spread + EPS)).astype(jnp.bfloat16)


def gelu_pair(pre, d_act):
    act, pullback = jax.vjp(lambda v: jax.nn.gelu(v, approximate=True), pre)
    return (act.astype(jnp.bfloat16), pullback(d_act)[0].astype(jnp.bfloat16))


def outer_sum(left, right):
    return lax.dot_general(
        left, right, (((0,), (0,)), ((), ())), preferred_element_type=jnp.float32
    )


def regroup(snap_params, first_moment, second_moment, range_of_writer):
    send_params = jnp.take(snap_params, range_of_writer, axis=0)
    send_first = jnp.take(first_moment, range_of_writer, axis=0)
    send_second = jnp.take(second_moment, range_of_writer, axis=0)
    written_params = lax.all_to_all(send_params, "group", split_axis=0, concat_axis=1, tiled=True)
    got_first, got_second = (
        lax.all_to_all(
            send_first.astype(jnp.bfloat16), "group", split_axis=0, concat_axis=1, tiled=True
        ).astype(send_first.dtype),
        lax.all_to_all(
            send_second.astype(jnp.bfloat16), "group", split_axis=0, concat_axis=1, tiled=True
        ).astype(send_second.dtype),
    )
    return (written_params, jnp.stack([got_first, got_second]))


def per_device(
    tokens,
    frame_mask,
    cotangent,
    up_weight,
    down_weight,
    snap_params,
    first_moment,
    second_moment,
    range_of_writer,
):
    written = regroup(snap_params, first_moment, second_moment, range_of_writer)
    normed = normalize(tokens)
    masked = cotangent * frame_mask[:, None].astype(jnp.bfloat16)
    hidden_cols = up_weight.shape[1]
    left = normed
    right = masked
    pre = jnp.dot(
        left,
        lax.all_gather(up_weight, "dp", axis=0, tiled=True),
        preferred_element_type=jnp.float32,
    )
    d_act = jnp.dot(
        right,
        lax.all_gather(down_weight, "dp", axis=0, tiled=True),
        preferred_element_type=jnp.float32,
    )
    act, grad_pre = gelu_pair(pre, d_act)
    left = normed
    right = masked
    summed = lax.psum_scatter(
        jnp.concatenate([outer_sum(left, grad_pre), outer_sum(right, act)], axis=1).astype(
            jnp.bfloat16
        ),
        "dp",
        scatter_dimension=0,
        tiled=True,
    ).astype(jnp.float32)
    grad_up = summed[:, :hidden_cols]
    grad_down = summed[:, hidden_cols:]
    return (grad_up, grad_down, written[0], written[1])


def solution(mesh):
    placed = (
        P("dp", None),
        P("dp"),
        P("dp", None),
        P("dp", "group"),
        P("dp", "group"),
        P(None, ("dp", "group")),
        P(None, ("dp", "group")),
        P(None, ("dp", "group")),
        P(),
    )
    return jax.shard_map(
        per_device,
        mesh=mesh,
        in_specs=placed,
        out_specs=(P("dp", "group"), P("dp", "group"), P("group", "dp"), P(None, "group", "dp")),
        check_vma=False,
    )
```

profile of v0, /device:TPU:0, one launch (start us, length us, event | category | flops | bytes accessed | tf_op | source)
XLA Modules:
  0.0 468.0 jit_solution(11517369713372826682)
XLA Ops:
  7.2 0.0 copy-start
  7.2 0.0 copy-start.4
  7.2 0.0 all-gather.5.cloned.1.call-start
  7.2 0.7 all-gather.5.cloned.1.call-update
  7.9 0.0 all-gather.3.cloned.1.call-start
  8.0 0.7 all-gather.3.cloned.1.call-update
  8.7 0.0 reduce-scatter.2.cloned.1.call-start
  8.7 0.0 copy-done.4
  8.7 0.0 copy-start.1
  8.8 3.4 convert_reduce_fusion
  12.2 0.6 copy-done.1
  12.8 1.5 fusion.2
  14.3 103.2 %all-gather.5.cloned.1.call-done = bf16[5120,1024]{1,0:T(8,128)(2,1)} async-done(((bf16[1280,1024]{1,0:T(8,128)(2,1)}), bf16[5120,1024]{1,0:T(8,128)(2,1)}) %all-gather.5.cloned.1.call-update) | async-done | bytes 10485776 | tf_op jit(solution)/shard_map/all_gather | solution.py:62
  117.5 9.9 %fusion.29 = f32[512,1024]{1,0:T(8,128)S(1)} fusion(bf16[5120,1024]{1,0:T(8,128)(2,1)} %all-gather.5.cloned.1.call-done, bf16[512,5120]{1,0:T(8,128)(2,1)} %param.11, f32[512]{0:T(512)S(1)} %add_rsqrt_fusion, f32[512]{0:T(512)S(1)} %broadcast_multiply_fusion), kind=kOutput, calls=%fused_computation.46 | convolution fusion | flops 5379194880 | bytes 17829888 | tf_op jit(solution)/shard_map/dot_general | solution.py:60
  127.5 11.7 %convolution_convert_fusion = bf16[5120,1024]{0,1:T(8,128)(2,1)} fusion(bf16[512,5120]{1,0:T(8,128)(2,1)} %param.13, bf16[512]{0:T(512)(128)(2,1)S(1)} %convert_element_type.54, f32[512,1024]{1,0:T(8,128)S(1)} %fusion.29), kind=kOutput, calls=%fused_computation.10 | convolution fusion | flops 5381292032 | bytes 17826816 | tf_op jit(solution)/shard_map/dot_general | solution.py:22
  139.1 85.2 %all-gather.3.cloned.1.call-done = bf16[5120,1024]{1,0:T(8,128)(2,1)} async-done(((bf16[1280,1024]{1,0:T(8,128)(2,1)}), bf16[5120,1024]{1,0:T(8,128)(2,1)}) %all-gather.3.cloned.1.call-update) | async-done | bytes 10485776 | tf_op jit(solution)/shard_map/all_gather | solution.py:67
  224.3 0.0 slice-start
  224.3 0.0 slice-start.1
  224.3 11.9 %fusion.15 = bf16[512,1024]{1,0:T(8,128)(2,1)S(1)} fusion(f32[512,1024]{1,0:T(8,128)S(1)} %fusion.29, bf16[5120,1024]{1,0:T(8,128)(2,1)} %all-gather.3.cloned.1.call-done, bf16[512,5120]{1,0:T(8,128)(2,1)} %param.13, bf16[512]{0:T(512)(128)(2,1)S(1)} %convert_element_type.54), kind=kOutput, calls=%fused_computation.25 | convolution fusion | flops 5381816320 | bytes 18875392 | tf_op jit(solution)/shard_map/dot_general | solution.py:65
  236.2 0.0 slice-start.2
  236.2 9.0 %convolution_convert_fusion.1 = bf16[5120,1024]{0,1:T(8,128)(2,1)S(1)} fusion(bf16[512,1024]{1,0:T(8,128)(2,1)S(1)} %fusion.15, bf16[512,5120]{1,0:T(8,128)(2,1)} %param.11, f32[512]{0:T(512)S(1)} %add_rsqrt_fusion, f32[512]{0:T(512)S(1)} %broadcast_multiply_fusion), kind=kOutput, calls=%fused_computation.11 | convolution fusion | flops 5384437760 | bytes 16781312 | tf_op jit(solution)/shard_map/dot_general | solution.py:22
  245.2 0.0 slice-done
  245.2 0.0 slice-done.1
  245.3 0.0 slice-done.2
  245.3 9.1 %pad_maximum_fusion = bf16[5120,2048]{0,1:T(8,128)(2,1)} fusion(bf16[5120,1024]{0,1:T(8,128)(2,1)S(1)} %bitcast.13, bf16[5120,1024]{0,1:T(8,128)(2,1)S(1)} %convolution_convert_fusion.1), kind=kLoop, calls=%fused_computation.3 | loop fusion | flops 41943040 | bytes 41943040 | tf_op jit(solution)/shard_map/concatenate | solution.py:74
  254.4 0.0 copy-start.5
  254.4 0.0 copy-start.3
  254.4 0.0 copy-start.2
  254.4 0.0 reduce-scatter.2.cloned.1.call-update
  254.4 0.6 copy-done.5
  255.0 0.0 copy-done
  255.0 0.6 gather_fusion.1
  255.6 0.0 copy-done.3
  255.6 0.6 gather_fusion.2
  256.2 0.1 fusion.22
  256.3 0.5 broadcast.123
  256.8 0.7 reduce.2
  257.5 0.6 reshape.139
  258.1 4.6 all-to-all-start.1
  262.7 0.7 reduce.1
  263.3 0.6 reshape.137
  264.0 0.0 copy-done.2
  264.0 0.6 gather_fusion
  264.5 3.8 all-to-all-done.1
  268.3 3.3 all-to-all-start.2
  271.7 0.1 bitcast_select_fusion
  271.8 0.7 reduce
  272.4 0.6 reshape.135
  273.1 4.2 all-to-all-done.2
  277.3 3.3 all-to-all-start
  280.7 5.5 %all-to-all-done = bf16[8,2,512]{2,1,0:T(2,128)(2,1)S(1)} async-done(((bf16[8,2,512]{2,1,0:T(2,128)(2,1)}), bf16[8,2,512]{2,1,0:T(2,128)(2,1)S(1)}, u32[]{:S(2)}, u32[]{:S(2)}) %all-to-all-start) | async-done | bytes 16416 | tf_op jit(solution)/shard_map/all_to_all | solution.py:31
  286.2 0.6 reshape.136
  286.8 0.7 maximum_convert_fusion
  287.6 154.8 %reduce-scatter.2.cloned.1.call-done = bf16[1280,2048]{0,1:T(8,128)(2,1)} async-done(((bf16[5120,2048]{0,1:T(8,128)(2,1)}), bf16[1280,2048]{0,1:T(8,128)(2,1)}) %reduce-scatter.2.cloned.1.call-update) | async-done | bytes 5242896 | tf_op jit(solution)/shard_map/reduce_scatter | solution.py:73
  442.3 7.4 %fusion.31 = (f32[1280,1024]{0,1:T(8,128)}, f32[1280,1024]{0,1:T(8,128)}) fusion(bf16[1280,2048]{0,1:T(8,128)(2,1)} %reduce-scatter.2.cloned.1.call-done), kind=kLoop, calls=%fused_computation.47 | loop fusion | bytes 20971520 | tf_op jit(solution)/shard_map/slice | solution.py:82
  449.7 5.9 %copy.18 = f32[1280,1024]{1,0:T(8,128)} copy(f32[1280,1024]{0,1:T(8,128)} %get-tuple-element.14) | data formatting | bytes 10485760
  455.6 5.9 %copy.19 = f32[1280,1024]{1,0:T(8,128)} copy(f32[1280,1024]{0,1:T(8,128)} %get-tuple-element.13) | data formatting | bytes 10485760
  (9 shorter events, 0.1 us)
Async XLA Ops:
  7.2 247.9 %copy-start = (f32[8,1024]{1,0:T(8,128)S(1)}, f32[8,1024]{1,0:T(8,128)}, u32[]{:S(2)}) copy-start(f32[8,1024]{1,0:T(8,128)} %param.17) | copy-start | bytes 98308
  7.2 1.5 copy-start.4
  7.2 110.3 %all-gather.5.cloned.1.call-start = ((), (), s32[]{:S(2)}) async-start(), calls=%async_computation.5 | async-start | bytes 13107200 | tf_op jit(solution)/shard_map/all_gather | solution.py:62
  7.9 216.4 %all-gather.3.cloned.1.call-start = ((), (), s32[]{:S(2)}) async-start(), calls=%async_computation.4 | async-start | bytes 13107200 | tf_op jit(solution)/shard_map/all_gather | solution.py:67
  8.7 433.6 %reduce-scatter.2.cloned.1.call-start = ((), (), s32[]{:S(2)}) async-start(), calls=%async_computation.6 | async-start | bytes 26214400 | tf_op jit(solution)/shard_map/reduce_scatter | solution.py:73
  8.7 4.0 copy-start.1
  224.3 20.9 %slice-start = ((s8[10485760]{0:T(1024)(128)(4,1)}), s8[4194304]{0:T(1024)(128)(4,1)S(1)}, s32[]{:S(2)}) async-start(s8[10485760]{0:T(1024)(128)(4,1)} %bitcast.12), calls=%async_computation.7 | async-start | bytes 8388608
  224.3 20.9 %slice-start.1 = ((s8[10485760]{0:T(1024)(128)(4,1)}), s8[4194304]{0:T(1024)(128)(4,1)S(1)}, s32[]{:S(2)}) async-start(s8[10485760]{0:T(1024)(128)(4,1)} %bitcast.12), calls=%async_computation.8 | async-start | bytes 8388608
  236.2 9.0 %slice-start.2 = ((s8[10485760]{0:T(1024)(128)(4,1)}), s8[2097152]{0:T(1024)(128)(4,1)S(1)}, s32[]{:S(2)}) async-start(s8[10485760]{0:T(1024)(128)(4,1)} %bitcast.12), calls=%async_computation.9 | async-start | bytes 4194304
  254.4 0.7 copy-start.5
  254.4 1.2 copy-start.3
  254.4 9.6 %copy-start.2 = (bf16[8,1024]{1,0:T(8,128)(2,1)S(1)}, bf16[8,1024]{1,0:T(8,128)(2,1)}, u32[]{:S(2)}) copy-start(bf16[8,1024]{1,0:T(8,128)(2,1)} %param.16) | copy-start | bytes 49156
  258.1 10.3 %all-to-all-start.1 = ((bf16[8,2,512]{2,1,0:T(2,128)(2,1)}), bf16[8,2,512]{2,1,0:T(2,128)(2,1)S(1)}, u32[]{:S(2)}, u32[]{:S(2)}) async-start(bf16[8,2,512]{2,1,0:T(2,128)(2,1)} %reshape.139), calls=%async_computation.2 | async-start | bytes 32768 | tf_op jit(solution)/shard_map/all_to_all | solution.py:33
  268.3 8.9 %all-to-all-start.2 = ((bf16[8,2,512]{2,1,0:T(2,128)(2,1)}), bf16[8,2,512]{2,1,0:T(2,128)(2,1)S(1)}, u32[]{:S(2)}, u32[]{:S(2)}) async-start(bf16[8,2,512]{2,1,0:T(2,128)(2,1)} %reshape.137), calls=%async_computation.3 | async-start | bytes 32768 | tf_op jit(solution)/shard_map/all_to_all | solution.py:36
  277.3 8.9 %all-to-all-start = ((bf16[8,2,512]{2,1,0:T(2,128)(2,1)}), bf16[8,2,512]{2,1,0:T(2,128)(2,1)S(1)}, u32[]{:S(2)}, u32[]{:S(2)}) async-start(bf16[8,2,512]{2,1,0:T(2,128)(2,1)} %reshape.135), calls=%async_computation.1 | async-start | bytes 32768 | tf_op jit(solution)/shard_map/all_to_all | solution.py:31
Sparse Core Ops, SparseCore 0:
  9.8 107.6 all-gather.4
  119.4 104.9 all-gather.2
  254.5 187.7 reduce-scatter.1
where the time goes:
time: 469 us; the launch traced here: 468 us
  waiting for transfers between devices  358 us (76%)
  matrix products  42.5 us (9%)
  local copies, waits for them, and re-layouts  25.2 us (5%)
  other arithmetic  16.9 us (4%)
  between operations  13.9 us (3%)
  starting transfers between devices  11.4 us (2%)
    reduce_scatter x1, waiting for transfers between devices, per_device(): lax.psum_scatter(jnp.concatenate([outer_sum(left, grad_pre), outer_sum(ri...  155 us
    all_gather x1, waiting for transfers between devices, per_device(): lax.all_gather(up_weight, 'dp', axis=0, tiled=True)  103 us
    all_gather x1, waiting for transfers between devices, per_device(): lax.all_gather(down_weight, 'dp', axis=0, tiled=True)  85.2 us
    dot_general x2, matrix products, outer_sum(): lax.dot_general(left, right, (((0,), (0,)), ((), ())), preferred_element_...  20.7 us
    unnamed x26, local copies, waits for them, and re-layouts  15.6 us
    dot_general x1, matrix products, per_device(): jnp.dot(right, lax.all_gather(down_weight, 'dp', axis=0, tiled=True), pre...  11.9 us
    dot_general x1, matrix products, per_device(): jnp.dot(left, lax.all_gather(up_weight, 'dp', axis=0, tiled=True), prefer...  9.93 us
  transfers between devices with their start and end apart: 6, of which 6 were waited for; matrix products, arithmetic and copies ran while one was open for 7% of the time, Pallas kernels for 0%

commit v1 on v0

v1 whole, which is shorter than its diff:
```python
import jax
import jax.numpy as jnp
from jax import lax
from jax.sharding import PartitionSpec as P

EPS = 1e-06


def normalize(tokens):
    values = tokens.astype(jnp.float32)
    centred = values - jnp.mean(values, axis=1, keepdims=True)
    spread = jnp.mean(centred * centred, axis=1, keepdims=True)
    return (centred * lax.rsqrt(spread + EPS)).astype(jnp.bfloat16)


def gelu_pair(pre, d_act):
    act, pullback = jax.vjp(lambda v: jax.nn.gelu(v, approximate=True), pre)
    return (act.astype(jnp.bfloat16), pullback(d_act)[0].astype(jnp.bfloat16))


def outer_sum(left, right):
    return lax.dot_general(
        left, right, (((0,), (0,)), ((), ())), preferred_element_type=jnp.float32
    )


def regroup(snap_params, first_moment, second_moment, range_of_writer):
    flat = snap_params.shape[1]
    held = jnp.concatenate(
        [snap_params, first_moment.astype(jnp.bfloat16), second_moment.astype(jnp.bfloat16)],
        axis=1,
    )
    send = jnp.take(held, range_of_writer, axis=0).reshape(-1, 3, flat)
    got = lax.all_to_all(send, "group", split_axis=0, concat_axis=0, tiled=True)
    lines = jnp.swapaxes(got, 0, 1).reshape(3, 1, -1)
    return lines[0], lines[1:].astype(first_moment.dtype)


def per_device(
    tokens,
    frame_mask,
    cotangent,
    up_weight,
    down_weight,
    snap_params,
    first_moment,
    second_moment,
    range_of_writer,
):
    written = regroup(snap_params, first_moment, second_moment, range_of_writer)
    rows = tokens.shape[0] // lax.axis_size("group")
    first = lax.axis_index("group") * rows
    own_tokens = lax.dynamic_slice_in_dim(tokens, first, rows, axis=0)
    own_mask = lax.dynamic_slice_in_dim(frame_mask, first, rows, axis=0)
    own_cotangent = lax.dynamic_slice_in_dim(cotangent, first, rows, axis=0)
    normed = normalize(own_tokens)
    masked = own_cotangent * own_mask[:, None].astype(jnp.bfloat16)

    def to_features(rows_here):
        part = lax.all_to_all(rows_here, "dp", split_axis=1, concat_axis=0, tiled=True)
        return lax.all_gather(part, "group", axis=0, tiled=True)

    def own_rows_total(left, weight):
        part = jnp.dot(left, weight, preferred_element_type=jnp.float32).astype(jnp.bfloat16)
        return lax.psum_scatter(part, "dp", scatter_dimension=0, tiled=True)

    normed = to_features(normed)
    masked = to_features(masked)
    pre = own_rows_total(normed, up_weight)
    d_act = own_rows_total(masked, down_weight)
    act, grad_pre = gelu_pair(pre.astype(jnp.float32), d_act.astype(jnp.float32))
    grad_down = outer_sum(masked, lax.all_gather(act, "dp", axis=0, tiled=True))
    grad_up = outer_sum(normed, lax.all_gather(grad_pre, "dp", axis=0, tiled=True))
    return (grad_up, grad_down, written[0], written[1])


def solution(mesh):
    placed = (
        P("dp", None),
        P("dp"),
        P("dp", None),
        P("dp", "group"),
        P("dp", "group"),
        P(None, ("dp", "group")),
        P(None, ("dp", "group")),
        P(None, ("dp", "group")),
        P(),
    )
    return jax.shard_map(
        per_device,
        mesh=mesh,
        in_specs=placed,
        out_specs=(P("dp", "group"), P("dp", "group"), P("group", "dp"), P(None, "group", "dp")),
        check_vma=False,
    )
```

time: 469 us -> 380 us (0.81)
  waiting for transfers between devices: 358 us -> 274 us
  blocking collectives: 0 us -> 37.2 us
  local copies, waits for them, and re-layouts: 25.2 us -> 2.06 us
  starting transfers between devices: 11.4 us -> 0.25 us
  other arithmetic: 16.9 us -> 10.8 us
    reduce_scatter x1 -> x2, waiting for transfers between devices: 155 us -> 101 us  [own_rows_total(): return lax.psum_scatter(part, 'dp', scatter_dimension=0, tiled=True)]
    all_to_all x0 -> x3, blocking collectives: none -> 37.2 us  [the longest x2 26.8 us: to_features(): lax.all_to_all(rows_here, 'dp', split_axis=1, concat_axis=0, tiled=True)]
    all_gather x2 -> x4, waiting for transfers between devices: 188 us -> 173 us  [the longest x2 88.6 us: to_features(): return lax.all_gather(part, 'group', axis=0, tiled=True)]
    unnamed x26 -> x11, local copies, waits for them, and re-layouts: 15.6 us -> 0.71 us
    all_to_all x3 -> x0, waiting for transfers between devices: 13.6 us -> none  [the longest x1 5.54 us: regroup(): lax.all_to_all(send_params, 'group', split_axis=0, concat_axis=1, tiled=T...]
    all_to_all x3 -> x0, starting transfers between devices: 11.3 us -> none  [the longest x1 4.61 us: regroup(): lax.all_to_all(send_first.astype(jnp.bfloat16), 'group', split_axis=0, co...]
    concatenate x1, other arithmetic: 9.1 us -> 0.01 us  [regroup(): jnp.concatenate([snap_params, first_moment.astype(jnp.bfloat16), second_m...]
    slice x1 -> x2, local copies, waits for them, and re-layouts: 7.43 us -> 0.68 us  [regroup(): return (lines[0], lines[1:].astype(first_moment.dtype))]
  transfers between devices with their start and end apart: 6 -> 6, of which waited for: 6 -> 6; matrix products, arithmetic and copies ran while one was open for 7% -> 9% of each run, Pallas kernels for 0% -> 0%
where the time goes in v1:
time: 380 us; the launch traced here: 379 us
  waiting for transfers between devices  274 us (72%)
  matrix products  40.2 us (11%)
  blocking collectives  37.2 us (10%)
  between operations  14.3 us (4%)
  other arithmetic  10.8 us (3%)
    reduce_scatter x2, waiting for transfers between devices, own_rows_total(): return lax.psum_scatter(part, 'dp', scatter_dimension=0, tiled=True)  101 us
    all_gather x2, waiting for transfers between devices, to_features(): return lax.all_gather(part, 'group', axis=0, tiled=True)  88.6 us
    all_gather x1, waiting for transfers between devices, per_device(): lax.all_gather(grad_pre, 'dp', axis=0, tiled=True)  44.6 us
    all_gather x1, waiting for transfers between devices, per_device(): grad_down = outer_sum(masked, lax.all_gather(act, 'dp', axis=0, tiled=True))  39.7 us
    all_to_all x2, blocking collectives, to_features(): lax.all_to_all(rows_here, 'dp', split_axis=1, concat_axis=0, tiled=True)  26.8 us
    dot_general x2, matrix products, outer_sum(): lax.dot_general(left, right, (((0,), (0,)), ((), ())), preferred_element_...  20.6 us
    dot_general x2, matrix products, own_rows_total(): jnp.dot(left, weight, preferred_element_type=jnp.float32)  19.6 us
    all_to_all x1, blocking collectives, regroup(): got = lax.all_to_all(send, 'group', split_axis=0, concat_axis=0, tiled=True)  10.3 us
  transfers between devices with their start and end apart: 6, of which 6 were waited for; matrix products, arithmetic and copies ran while one was open for 9% of the time, Pallas kernels for 0%

profile of v1, /device:TPU:0, one launch (start us, length us, event | category | flops | bytes accessed | tf_op | source)
XLA Modules:
  0.0 379.1 jit_solution(6365481262958353322)
XLA Ops:
  7.2 0.0 copy-start
  7.2 0.0 all-gather.5.cloned.1.call-start
  7.2 1.4 convert_reduce_fusion
  8.7 1.4 fusion.13
  10.1 1.3 fusion.14
  11.5 15.0 %all_to_all.43 = bf16[64,4,1280]{2,0,1:T(8,128)(2,1)} all-to-all(bf16[64,4,1280]{2,0,1:T(8,128)(2,1)S(1)} %bitcast.31), channel_id=1, replica_groups=mesh['dp'=4,'group'=8] {'dp'}, dimensions={1} | all-to-all | bytes 1310720 | tf_op jit(solution)/shard_map/all_to_all | solution.py:60
  26.5 0.0 all-gather.5.cloned.1.call-update
  26.5 0.0 all-gather.7.cloned.1.call-start
  26.6 0.8 dynamic-slice_convert_fusion
  27.3 1.3 dynamic-slice_multiply_fusion
  28.7 11.8 %all_to_all.44 = bf16[64,4,1280]{2,0,1:T(8,128)(2,1)} all-to-all(bf16[64,4,1280]{2,0,1:T(8,128)(2,1)S(1)} %bitcast.32), channel_id=1, replica_groups=mesh['dp'=4,'group'=8] {'dp'}, dimensions={1} | all-to-all | bytes 1310720 | tf_op jit(solution)/shard_map/all_to_all | solution.py:60
  40.5 0.0 all-gather.7.cloned.1.call-update
  40.5 0.0 reduce-scatter.5.cloned.1.call-start
  40.6 41.8 %all-gather.5.cloned.1.call-done = bf16[2048,1280]{1,0:T(8,128)(2,1)} async-done(((bf16[256,1280]{1,0:T(8,128)(2,1)}), bf16[2048,1280]{1,0:T(8,128)(2,1)}) %all-gather.5.cloned.1.call-update) | async-done | bytes 5242896 | tf_op jit(solution)/shard_map/all_gather | solution.py:61
  82.4 0.0 copy-done
  82.4 9.6 %convolution_convert_fusion = bf16[2048,1024]{1,0:T(8,128)(2,1)} fusion(bf16[2048,1280]{1,0:T(8,128)(2,1)} %all-gather.5.cloned.1.call-done, bf16[1280,1024]{1,0:T(8,128)(2,1)S(1)} %copy-done), kind=kOutput, calls=%fused_computation.6 | convolution fusion | flops 5370806272 | bytes 12058624 | tf_op jit(solution)/shard_map/dot_general | solution.py:64
  92.0 0.0 reduce-scatter.5.cloned.1.call-update
  92.0 0.0 reduce-scatter.3.cloned.1.call-start
  92.1 46.7 %all-gather.7.cloned.1.call-done = bf16[2048,1280]{1,0:T(8,128)(2,1)} async-done(((bf16[256,1280]{1,0:T(8,128)(2,1)}), bf16[2048,1280]{1,0:T(8,128)(2,1)}) %all-gather.7.cloned.1.call-update) | async-done | bytes 5242896 | tf_op jit(solution)/shard_map/all_gather | solution.py:61
  138.8 10.0 %convolution_convert_fusion.1 = bf16[2048,1024]{1,0:T(8,128)(2,1)} fusion(bf16[2048,1280]{1,0:T(8,128)(2,1)} %all-gather.7.cloned.1.call-done, bf16[1280,1024]{1,0:T(8,128)(2,1)} %param.13), kind=kOutput, calls=%fused_computation.7 | convolution fusion | flops 5370806272 | bytes 12058624 | tf_op jit(solution)/shard_map/dot_general | solution.py:64
  148.8 0.0 reduce-scatter.3.cloned.1.call-update
  148.8 0.0 copy-start.1
  148.8 0.0 copy-start.2
  148.9 0.0 copy-start.4
  148.9 0.0 copy-start.3
  148.9 0.0 all-gather.11.cloned.1.call-start
  148.9 44.8 %reduce-scatter.5.cloned.1.call-done = bf16[512,1024]{1,0:T(8,128)(2,1)} async-done(((bf16[2048,1024]{1,0:T(8,128)(2,1)}), bf16[512,1024]{1,0:T(8,128)(2,1)}) %reduce-scatter.5.cloned.1.call-update) | async-done | bytes 1048592 | tf_op jit(solution)/shard_map/reduce_scatter | solution.py:65
  193.8 56.0 %reduce-scatter.3.cloned.1.call-done = bf16[512,1024]{1,0:T(8,128)(2,1)} async-done(((bf16[2048,1024]{1,0:T(8,128)(2,1)}), bf16[512,1024]{1,0:T(8,128)(2,1)}) %reduce-scatter.3.cloned.1.call-update) | async-done | bytes 1048592 | tf_op jit(solution)/shard_map/reduce_scatter | solution.py:65
  249.8 4.5 %fusion.10 = (bf16[512,1024]{1,0:T(8,128)(2,1)}, bf16[512,1024]{1,0:T(8,128)(2,1)}) fusion(bf16[512,1024]{1,0:T(8,128)(2,1)} %reduce-scatter.5.cloned.1.call-done, bf16[512,1024]{1,0:T(8,128)(2,1)} %reduce-scatter.3.cloned.1.call-done), kind=kLoop, calls=%fused_computation.19 | loop fusion | flops 12582912 | bytes 4194304 | tf_op jit(solution)/shard_map/convert_element_type | solution.py:18
  254.3 0.0 all-gather.11.cloned.1.call-update
  254.3 0.0 all-gather.9.cloned.1.call-start
  254.4 0.5 all-gather.9.cloned.1.call-update
  254.9 0.0 copy-done.1
  254.9 0.0 copy-done.2
  254.9 0.0 copy-done.4
  255.0 0.0 copy-done.3
  255.0 0.6 gather_fusion
  255.6 0.1 copy_select_fusion
  255.7 10.3 %all_to_all.45 = bf16[8,3,1024]{2,1,0:T(4,128)(2,1)S(1)} all-to-all(bf16[8,3,1024]{2,1,0:T(4,128)(2,1)S(1)} %copy_select_fusion), channel_id=1, replica_groups=mesh['dp'=4,'group'=8] {'group'}, dimensions={0} | all-to-all | bytes 98304 | tf_op jit(solution)/shard_map/all_to_all | solution.py:34
  266.1 0.6 slice.12
  266.7 0.7 copy.21
  267.4 39.7 %all-gather.11.cloned.1.call-done = bf16[2048,1024]{1,0:T(8,128)(2,1)} async-done(((bf16[512,1024]{1,0:T(8,128)(2,1)}), bf16[2048,1024]{1,0:T(8,128)(2,1)}) %all-gather.11.cloned.1.call-update) | async-done | bytes 4194320 | tf_op jit(solution)/shard_map/all_gather | solution.py:72
  307.1 10.3 %fusion.16 = f32[1280,1024]{1,0:T(8,128)} fusion(bf16[2048,1280]{1,0:T(8,128)(2,1)} %all-gather.7.cloned.1.call-done, bf16[2048,1024]{1,0:T(8,128)(2,1)} %all-gather.11.cloned.1.call-done), kind=kOutput, calls=%fused_computation.38 | convolution fusion | flops 5368709120 | bytes 14680064 | tf_op jit(solution)/shard_map/dot_general | solution.py:22
  317.4 44.6 %all-gather.9.cloned.1.call-done = bf16[2048,1024]{1,0:T(8,128)(2,1)} async-done(((bf16[512,1024]{1,0:T(8,128)(2,1)}), bf16[2048,1024]{1,0:T(8,128)(2,1)}) %all-gather.9.cloned.1.call-update) | async-done | bytes 4194320 | tf_op jit(solution)/shard_map/all_gather | solution.py:73
  361.9 10.3 %fusion.15 = f32[1280,1024]{1,0:T(8,128)} fusion(bf16[2048,1280]{1,0:T(8,128)(2,1)} %all-gather.5.cloned.1.call-done, bf16[2048,1024]{1,0:T(8,128)(2,1)} %all-gather.9.cloned.1.call-done), kind=kOutput, calls=%fused_computation.37 | convolution fusion | flops 5368709120 | bytes 14680064 | tf_op jit(solution)/shard_map/dot_general | solution.py:22
  (11 shorter events, 0.2 us)
Async XLA Ops:
  7.2 75.2 %copy-start = (bf16[1280,1024]{1,0:T(8,128)(2,1)S(1)}, bf16[1280,1024]{1,0:T(8,128)(2,1)}, u32[]{:S(2)}) copy-start(bf16[1280,1024]{1,0:T(8,128)(2,1)} %param.12) | copy-start | bytes 7864324
  7.2 75.2 %all-gather.5.cloned.1.call-start = ((), (), s32[]{:S(2)}) async-start(), calls=%async_computation.5 | async-start | bytes 5898240 | tf_op jit(solution)/shard_map/all_gather | solution.py:61
  26.5 112.3 %all-gather.7.cloned.1.call-start = ((), (), s32[]{:S(2)}) async-start(), calls=%async_computation.6 | async-start | bytes 5898240 | tf_op jit(solution)/shard_map/all_gather | solution.py:61
  40.5 153.2 %reduce-scatter.5.cloned.1.call-start = ((), (), s32[]{:S(2)}) async-start(), calls=%async_computation.8 | async-start | bytes 5242880 | tf_op jit(solution)/shard_map/reduce_scatter | solution.py:65
  92.0 157.8 %reduce-scatter.3.cloned.1.call-start = ((), (), s32[]{:S(2)}) async-start(), calls=%async_computation.7 | async-start | bytes 5242880 | tf_op jit(solution)/shard_map/reduce_scatter | solution.py:65
  148.8 106.1 %copy-start.1 = (f32[8,1024]{1,0:T(8,128)S(1)}, f32[8,1024]{1,0:T(8,128)}, u32[]{:S(2)}) copy-start(f32[8,1024]{1,0:T(8,128)} %param.15) | copy-start | bytes 98308
  148.8 106.1 %copy-start.2 = (f32[8,1024]{1,0:T(8,128)S(1)}, f32[8,1024]{1,0:T(8,128)}, u32[]{:S(2)}) copy-start(f32[8,1024]{1,0:T(8,128)} %param.16) | copy-start | bytes 98308
  148.9 106.1 %copy-start.4 = (s32[8]{0:T(128)S(1)}, s32[8]{0:T(128)}, u32[]{:S(2)}) copy-start(s32[8]{0:T(128)} %param.17) | copy-start | bytes 100
  148.9 106.1 %copy-start.3 = (bf16[8,1024]{1,0:T(8,128)(2,1)S(1)}, bf16[8,1024]{1,0:T(8,128)(2,1)}, u32[]{:S(2)}) copy-start(bf16[8,1024]{1,0:T(8,128)(2,1)} %param.14) | copy-start | bytes 49156
  148.9 158.2 %all-gather.11.cloned.1.call-start = ((), (), s32[]{:S(2)}) async-start(), calls=%async_computation.10 | async-start | bytes 5242880 | tf_op jit(solution)/shard_map/all_gather | solution.py:72
  254.3 107.6 %all-gather.9.cloned.1.call-start = ((), (), s32[]{:S(2)}) async-start(), calls=%async_computation.9 | async-start | bytes 5242880 | tf_op jit(solution)/shard_map/all_gather | solution.py:73
Sparse Core Ops, SparseCore 0:
  26.7 55.6 all-gather.4
  84.0 54.7 all-gather.6
  142.3 51.3 reduce-scatter.4
  197.2 52.5 reduce-scatter.2
  254.4 52.5 all-gather.10
  309.3 52.5 all-gather.8
